TPU v7x, 256 devices: a whole 4x4x8 slice. The times are simulated.
256 devices in a mesh: seq: 16 (over z, core), head: 16 (over x, y).
Axes of the slice: x: 4, y: 4, z: 8, core: 2. Of those that a mesh axis runs over, the one named last changes fastest.
Arguments:
- grad_output: bfloat16 [16384, 4096], P('seq', 'head'), may hold values from -6 to 6
- out_weight: bfloat16 [4096, 8192], P('seq', 'head'), may hold values from -0.0625 to 0.0625
- ssd_out: bfloat16 [16384, 8192], P('seq', 'head'), may hold values from -520 to 520
- gate: bfloat16 [16384, 8192], P('seq', 'head'), may hold values from -5 to 5
- norm_weight: float32 [8192], P('head'), may hold values from 0.5 to 1.5
- time_step: float32 [128, 16384], P('head', 'seq'), may hold values from 0.01 to 0.1
- log_decay: float32 [128, 16384], P('head', 'seq'), may hold values from -0.7 to 0
- state_in: bfloat16 [16384, 8, 128], P('seq'), may hold values from -1.796875 to 1.796875
- state_out: bfloat16 [16384, 8, 128], P('seq'), may hold values from -1.796875 to 1.796875
- skip: float32 [128], P('head'), may hold values from 0.5 to 1.5
Outputs:
- grad_x: bfloat16 [16384, 8192], P('seq', 'head')
- grad_gate: bfloat16 [16384, 8192], P('seq', 'head')
- grad_out_weight: float32 [4096, 8192], P('seq', 'head')
All inputs are finite; a program needn't handle non-finite values.
Results may differ from a plain program's by a relative error of at most 0.014.
Values may be sent and summed in bfloat16 or wider, within the bound.
A program may use at most 128 MiB of HBM per device.

v0:
```python
import math
import jax
import jax.numpy as jnp
from jax import lax
from jax.sharding import Mesh
from jax.sharding import PartitionSpec as P

HEADS = 128
GROUPS = 8
BLOCK_LEN = 256
HEAD = ("head_0", "head_1")
SEQ = ("seq_0", "seq_1")
epsilon = 1e-05


def over_axes(x, axes):
    for axis in axes:
        x = lax.psum(x, axis)
    return x


def nothing_yet(x, identity):
    return jax.tree.map(
        lambda part, zero: jnp.zeros_like(part) + jnp.asarray(zero, part.dtype), x, identity
    )


def carried_in(x, axes, combine, identity):
    before = start = nothing_yet(x, identity)
    running = x
    for axis in reversed(axes):
        size, here = (lax.axis_size(axis), lax.axis_index(axis))
        pieces = jax.tree.map(lambda part: lax.all_gather(part, axis), running)
        inside, running = (start, start)
        for k in reversed(range(size)):
            passed = k > here
            running = combine(running, jax.tree.map(lambda part: part[k], pieces))
            inside = jax.tree.map(lambda new, old: jnp.where(passed, new, old), running, inside)
        before = combine(inside, before)
    return before


def on_device(
    grad_output,
    out_weight,
    ssd_out,
    gate,
    norm_weight,
    time_step,
    log_decay,
    state_in,
    state_out,
    skip,
):
    tok_rows = ssd_out.shape[0]
    local_width = ssd_out.shape[1]
    total_width = local_width * lax.axis_size(HEAD)
    full_grad = lax.all_gather(grad_output, HEAD, axis=1, tiled=True)
    values = ssd_out.astype(jnp.float32)
    gate_values = gate.astype(jnp.float32)
    sigmoid_gate = jax.nn.sigmoid(gate_values)
    silu_gate = gate_values * sigmoid_gate
    gated_values = values * silu_gate
    local_squares = jnp.sum(gated_values * gated_values, axis=1)
    columns = full_grad
    normed_grad = jnp.dot(
        columns,
        lax.all_gather(out_weight, SEQ, axis=0, tiled=True),
        preferred_element_type=jnp.float32,
    )
    squares = over_axes(local_squares, HEAD)
    weighted = over_axes(jnp.sum(norm_weight * normed_grad * gated_values, axis=1), HEAD)
    inverse_rms = lax.rsqrt(squares[:, None] / total_width + epsilon)
    normed = (gated_values * inverse_rms * norm_weight).astype(jnp.bfloat16)
    gated_grad = (
        inverse_rms * norm_weight * normed_grad
        - gated_values * inverse_rms**3 * weighted[:, None] / total_width
    )
    grad_gate = (
        gated_grad * values * sigmoid_gate * (1.0 + gate_values * (1.0 - sigmoid_gate))
    ).astype(jnp.bfloat16)
    grad_ssd = (gated_grad * silu_gate).astype(jnp.bfloat16)
    columns = full_grad
    weight_sum = lax.psum_scatter(
        lax.dot_general(
            columns, normed, (((0,), (0,)), ((), ())), preferred_element_type=jnp.float32
        ).astype(jnp.bfloat16),
        SEQ,
        scatter_dimension=0,
        tiled=True,
    ).astype(jnp.float32)
    grad_out_weight = weight_sum * (1.0 / math.sqrt(tok_rows * lax.axis_size(SEQ)))
    heads_here = time_step.shape[0]
    head_width = local_width // heads_here
    blocks = tok_rows // BLOCK_LEN
    state_width = state_in.shape[2]
    group_count = state_in.shape[1]
    first_head = lax.axis_index(HEAD) * heads_here
    head_ids = first_head + jnp.arange(heads_here, dtype=jnp.int32)
    group_ids = head_ids // (HEADS // GROUPS)
    group_pick = (group_ids[:, None] == jnp.arange(group_count, dtype=jnp.int32)[None, :]).astype(
        jnp.bfloat16
    )
    b_heads = jnp.einsum(
        "tgn,hg->htn", state_in, group_pick, preferred_element_type=jnp.float32
    ).astype(jnp.bfloat16)
    b_heads = b_heads.reshape(heads_here, blocks, BLOCK_LEN, state_width)
    c_heads = jnp.einsum(
        "tgn,hg->htn", state_out, group_pick, preferred_element_type=jnp.float32
    ).astype(jnp.bfloat16)
    c_heads = c_heads.reshape(heads_here, blocks, BLOCK_LEN, state_width)
    grad_heads = grad_ssd.reshape(tok_rows, heads_here, head_width).transpose(1, 0, 2)
    grad_heads = grad_heads.reshape(heads_here, blocks, BLOCK_LEN, head_width)
    cumulative = jnp.cumsum(log_decay.reshape(heads_here, blocks, BLOCK_LEN), axis=2)
    block_total = cumulative[..., -1]
    sequence_indices = jnp.arange(BLOCK_LEN)
    upper_mask = sequence_indices[None, :] >= sequence_indices[:, None]
    scores = jnp.einsum("hktn,hksn->hkts", b_heads, c_heads, preferred_element_type=jnp.float32)
    log_gap = cumulative[..., None, :] - cumulative[..., :, None]
    block_weights = jnp.where(upper_mask, scores * jnp.exp(jnp.minimum(log_gap, 0.0)), 0.0).astype(
        jnp.bfloat16
    )
    within = jnp.einsum(
        "hkts,hksp->hktp", block_weights, grad_heads, preferred_element_type=jnp.float32
    )
    grad_float = grad_heads.astype(jnp.float32)
    scaled = (jnp.exp(cumulative)[..., None] * grad_float).astype(jnp.bfloat16)
    block_state = jnp.einsum("hksp,hksn->hkpn", scaled, c_heads, preferred_element_type=jnp.float32)

    def fold_block(carried, inputs):
        state_now, total_now = inputs
        return (state_now + jnp.exp(total_now)[:, None, None] * carried, carried)

    zero_state = jnp.zeros((heads_here, head_width, state_width), jnp.float32)
    summary, inside = lax.scan(
        fold_block, zero_state, (block_state.transpose(1, 0, 2, 3), block_total.T), reverse=True
    )
    decay_total = jnp.exp(jnp.sum(block_total, axis=1))
    tail_decay = jnp.exp(
        jnp.sum(block_total, axis=1, keepdims=True) - jnp.cumsum(block_total, axis=1)
    )

    def combine_pair(earlier, later):
        return (later[0] * earlier[0], later[1] + later[0][:, None, None] * earlier[1])

    identity = (jnp.ones((heads_here,), jnp.float32), zero_state)
    prefix = carried_in((decay_total, summary), SEQ, combine_pair, identity)
    remote = prefix[1]
    full_states = inside.transpose(1, 0, 2, 3) + tail_decay[..., None, None] * remote[:, None]
    carry_low = full_states.astype(jnp.bfloat16)
    across = jnp.einsum("hkpn,hktn->hktp", carry_low, b_heads, preferred_element_type=jnp.float32)
    across = across * jnp.exp(block_total[..., None] - cumulative)[..., None]
    step_sizes = time_step.reshape(heads_here, blocks, BLOCK_LEN)
    grad_head = step_sizes[..., None] * (within + across) + skip[:, None, None, None] * grad_float
    grad_x = (
        grad_head.reshape(heads_here, tok_rows, head_width)
        .transpose(1, 0, 2)
        .reshape(tok_rows, local_width)
    )
    return (grad_x.astype(jnp.bfloat16), grad_gate, grad_out_weight)


def solution(mesh):
    finer = Mesh(mesh.devices.reshape(8, 2, 4, 4), ("seq_0", "seq_1", "head_0", "head_1"))
    return jax.shard_map(
        on_device,
        mesh=finer,
        in_specs=(
            P(SEQ, HEAD),
            P(SEQ, HEAD),
            P(SEQ, HEAD),
            P(SEQ, HEAD),
            P(HEAD),
            P(HEAD, SEQ),
            P(HEAD, SEQ),
            P(SEQ, None, None),
            P(SEQ, None, None),
            P(HEAD),
        ),
        out_specs=(P(SEQ, HEAD), P(SEQ, HEAD), P(SEQ, HEAD)),
        check_vma=False,
    )
```

profile of v0, /device:TPU:2, one launch (start us, length us, event | category | flops | bytes accessed | tf_op | source)
XLA Modules:
  0.0 294.2 jit_solution(11251501523468864543)
XLA Ops:
  8.7 1.3 dynamic-slice.1
  13.3 2.3 reduce-window.6
  16.2 1.5 copy.74
  17.7 2.6 copy.75
  20.4 2.4 all-reduce
  23.1 2.1 convolution_convert_fusion.1
  25.2 29.5 %all-gather.9.cloned.1.call-done = bf16[4096,512]{1,0:T(8,128)(2,1)} async-done(((bf16[256,512]{1,0:T(8,128)(2,1)}), bf16[4096,512]{1,0:T(8,128)(2,1)}) %all-gather.9.cloned.1.call-update) | async-done | bytes 4194320 | tf_op jit(solution)/shard_map/all_gather | solution.py:68
  54.7 82.9 %all-gather.7.cloned.1.call-done = bf16[1024,4096]{1,0:T(8,128)(2,1)} async-done(((bf16[1024,256]{1,0:T(8,128)(2,1)}), bf16[1024,4096]{1,0:T(8,128)(2,1)}) %all-gather.7.cloned.1.call-update) | async-done | bytes 8388624 | tf_op jit(solution)/shard_map/all_gather | solution.py:58
  137.6 11.3 %multiply_reduce_fusion.1 = (f32[1024]{0:T(1024)S(1)}, f32[1024]{0:T(1024)S(1)}, f32[1024,512]{0,1:T(8,128)}) fusion(bf16[1024,512]{0,1:T(8,128)(2,1)S(1)} %copy.74, bf16[1024,512]{0,1:T(8,128)(2,1)} %copy.75, f32[512]{0:T(512)S(1)} %copy-done.7, bf16[1024,4096]{1,0:T(8,128)(2,1)} %all-gather.7.cloned.1.call-done, ...), kind=kOutput, calls=%fused_computation.32 | convolution fusion | flops 4301256704 | bytes 16787456 | tf_op jit(solution)/shard_map/dot_general | solution.py:66
  148.8 8.7 %all-reduce.3 = (f32[1024]{0:T(1024)S(1)}, f32[1024]{0:T(1024)S(1)}) all-reduce(f32[1024]{0:T(1024)S(1)} %get-tuple-element.160, f32[1024]{0:T(1024)S(1)} %get-tuple-element.159), channel_id=1, replica_groups=mesh['seq_0'=8,'seq_1'=2,'head_0'=4,'head_1'=4] {'head_0'}, use_global_device_ids=true, to_apply=%region_6.0 | all-reduce | flops 2048 | bytes 16384 | tf_op jit(solution)/shard_map/psum | solution.py:18
  157.5 10.2 %all-reduce.2 = (f32[1024]{0:T(1024)S(1)}, f32[1024]{0:T(1024)S(1)}) all-reduce(f32[1024]{0:T(1024)S(1)} %get-tuple-element.175, f32[1024]{0:T(1024)S(1)} %get-tuple-element.176), channel_id=1, replica_groups=mesh['seq_0'=8,'seq_1'=2,'head_0'=4,'head_1'=4] {'head_1'}, use_global_device_ids=true, to_apply=%region_7.8 | all-reduce | flops 2048 | bytes 16384 | tf_op jit(solution)/shard_map/psum | solution.py:18
  167.8 4.7 %fusion.9 = (bf16[1024,512]{0,1:T(8,128)(2,1)}, bf16[1024,512]{0,1:T(8,128)(2,1)S(1)}) fusion(bf16[1024,512]{0,1:T(8,128)(2,1)S(1)} %copy.74, bf16[1024,512]{0,1:T(8,128)(2,1)} %copy.75, f32[1024]{0:T(1024)S(1)} %get-tuple-element.173, f32[1024]{0:T(1024)S(1)} %get-tuple-element.182, f32[1024,512]{0,1:T(8,128)} %get-tuple-element.195, f32[512]{0:T(512)S(1)} %copy-done.7, ...), kind=kLoop, calls=%fused_computation.20 | loop fusion | flops 11534336 | bytes 6305792 | tf_op jit(solution)/shard_map/convert_element_type | solution.py:81
  172.5 1.8 fusion.27
  174.3 4.5 %while.17 = (s32[]{:T(128)}, f32[8,64,128]{2,1,0:T(8,128)S(1)}, f32[4,8,64,128]{3,2,1,0:T(8,128)S(1)}, f32[4,8,64,128]{3,2,0,1:T(8,128)}, f32[4,8]{1,0:T(4,128)S(1)}, /*index=5*/s32[]{:T(128)}, s32[]{:T(128)}, s32[]{:T(128)}) while((s32[]{:T(128)}, f32[8,64,128]{2,1,0:T(8,128)S(1)}, f32[4,8,64,128]{3,2,1,0:T(8,128)S(1)}, ...), condition=%wide.region_9.10_spmd.clone, body=%wide.region_8.9_spmd.clone.sunk | while | flops 262148 | bytes 1310944 | solution.py:135
  179.8 2.2 all-gather
  183.0 11.0 %fusion.2 = bf16[4096,512]{0,1:T(8,128)(2,1)} fusion(bf16[1024,4096]{1,0:T(8,128)(2,1)} %all-gather.7.cloned.1.call-done, f32[512]{0:T(512)S(1)} %copy-done.7, bf16[1024,512]{0,1:T(8,128)(2,1)} %copy-done.2, f32[1024]{0:T(1024)S(1)} %get-tuple-element.181, bf16[1024,512]{0,1:T(8,128)(2,1)} %copy.75), kind=kOutput, calls=%fused_computation.7 | convolution fusion | flops 4302307328 | bytes 14686208 | tf_op jit(solution)/shard_map/dot_general | solution.py:85
  194.9 17.7 %all-reduce.1 = f32[64]{0:T(128)S(1)} all-reduce(f32[64]{0:T(128)S(1)} %copy-done.10), channel_id=4, replica_groups=mesh['seq_0'=8,'seq_1'=2,'head_0'=4,'head_1'=4] {'seq_0'}, use_global_device_ids=true, to_apply=%add.1 | all-reduce | flops 64 | bytes 512
  212.7 3.7 %convolution_convert_fusion.2 = bf16[8,1024,128]{2,0,1:T(8,128)(2,1)} fusion(bf16[1024,8,128]{2,1,0:T(8,128)(2,1)} %param.19, s32[8]{0:T(128)S(1)} %and_select_fusion), kind=kOutput, calls=%fused_computation.34 | convolution fusion | flops 17825856 | bytes 4194336 | tf_op jit(solution)/shard_map/tgn,hg->htn/dot_general | solution.py:104
  216.3 2.3 copy.86
  218.6 6.3 %fusion.3 = f32[8,4,256,64]{2,3,1,0:T(8,128)} fusion(f32[8,4,256]{2,1,0:T(4,128)S(1)} %copy.72, pred[256,256]{1,0:T(8,128)(4,1)S(1)} %iota_compare_fusion, bf16[8,4,256,128]{3,0,2,1:T(8,128)(2,1)} %bitcast.136, bf16[8,4,256,128]{3,0,2,1:T(8,128)(2,1)} %bitcast.130, bf16[8,8,4,8,256]{4,3,2,1,0:T(8,128)(2,1)} %bitcast.133), kind=kOutput, calls=%fused_computation.8 | convolution fusion | flops 815792128 | bytes 7438336 | tf_op jit(solution)/shard_map/hkts,hksp->hktp/dot_general | solution.py:123
  224.9 2.1 fusion.53
  227.2 3.3 %fusion.30 = bf16[8,4,8,8,256]{4,3,2,1,0:T(8,128)(2,1)S(1)} fusion(f32[8,4,256,64]{2,3,1,0:T(8,128)} %fusion.3, bf16[8,4,256,128]{3,0,2,1:T(8,128)(2,1)S(1)} %bitcast.131, f32[8]{0:T(128)S(1)} %copy-done.8, f32[8,4,256]{2,1,0:T(4,128)S(1)} %copy.83, f32[8,4,256]{2,1,0:T(4,128)S(1)} %copy.67, bf16[8,8,4,8,256]{4,3,2,1,0:T(8,128)(2,1)} %bitcast.134, ...), kind=kOutput, calls=%fused_computation.42 | convolution fusion | flops 138674176 | bytes 7667872 | tf_op jit(solution)/shard_map/hkpn,hktn->hktp/dot_general | solution.py:151
  230.6 1.3 copy.85
  231.9 53.7 %reduce-scatter.2.cloned.1.call-done = bf16[256,512]{0,1:T(8,128)(2,1)} async-done(((bf16[4096,512]{0,1:T(8,128)(2,1)}), bf16[256,512]{0,1:T(8,128)(2,1)}) %reduce-scatter.2.cloned.1.call-update) | async-done | bytes 262160 | tf_op jit(solution)/shard_map/reduce_scatter | solution.py:84
  (71 shorter events, 14.0 us)
Async XLA Ops:
  7.2 15.9 %copy-start = (bf16[1024,8,128]{2,1,0:T(8,128)(2,1)S(1)}, bf16[1024,8,128]{2,1,0:T(8,128)(2,1)}, u32[]{:S(2)}) copy-start(bf16[1024,8,128]{2,1,0:T(8,128)(2,1)} %param.20) | copy-start | bytes 6291460
  7.2 47.5 %all-gather.9.cloned.1.call-start = ((), (), s32[]{:S(2)}) async-start(), calls=%async_computation.2 | async-start | bytes 4456448 | tf_op jit(solution)/shard_map/all_gather | solution.py:68
  7.9 129.7 %all-gather.7.cloned.1.call-start = ((), (), s32[]{:S(2)}) async-start(), calls=%async_computation.1 | async-start | bytes 8912896 | tf_op jit(solution)/shard_map/all_gather | solution.py:58
  8.7 216.3 %all-gather.11.cloned.1.call-start = ((), (), s32[]{:S(2)}) async-start(), calls=%async_computation.3 | async-start | bytes 2359296 | tf_op jit(solution)/shard_map/all_gather | solution.py:33
  17.7 150.1 %copy-start.2 = (bf16[1024,512]{0,1:T(8,128)(2,1)}, bf16[1024,512]{0,1:T(8,128)(2,1)S(1)}, u32[]{:S(2)}) copy-start(bf16[1024,512]{0,1:T(8,128)(2,1)S(1)} %copy.74) | copy-start | bytes 3145732
  23.1 2.1 copy-start.9
  23.1 114.5 %copy-start.7 = (f32[512]{0:T(512)S(1)}, f32[512]{0:T(512)}, u32[]{:S(2)}) copy-start(f32[512]{0:T(512)} %param.16) | copy-start | bytes 6148
  167.8 4.7 %copy-start.5 = (bf16[8,1024,128]{2,0,1:T(8,128)(2,1)S(1)}, bf16[8,1024,128]{2,0,1:T(8,128)(2,1)}, u32[]{:S(2)}) copy-start(bf16[8,1024,128]{2,0,1:T(8,128)(2,1)} %convolution_convert_fusion.1) | copy-start | bytes 6291460
  172.5 1.8 copy-start.3
  178.8 1.0 copy-start.4
  182.8 102.8 %reduce-scatter.2.cloned.1.call-start = ((), (), s32[]{:S(2)}) async-start(), calls=%async_computation.4 | async-start | bytes 4456448 | tf_op jit(solution)/shard_map/reduce_scatter | solution.py:84
  194.0 0.8 copy-start.6
  194.1 0.8 copy-start.10
  224.9 2.1 copy-start.8
  224.9 2.2 copy-start.1
Sparse Core Ops, SparseCore 0:
  9.8 44.8 all-gather.8
  57.1 80.4 all-gather.6
  182.9 38.5 all-gather.10
  223.9 61.6 reduce-scatter.1
where the time goes:
time: 295 us; the launch traced here: 294 us
  waiting for transfers between devices  167 us (57%)
  blocking collectives  41.2 us (14%)
  matrix products  39.5 us (13%)
  other arithmetic  15.8 us (5%)
  between operations  15.3 us (5%)
  local copies, waits for them, and re-layouts  14.4 us (5%)
    all_gather x1, waiting for transfers between devices, on_device(): full_grad = lax.all_gather(grad_output, HEAD, axis=1, tiled=True)  82.9 us
    reduce_scatter x1, waiting for transfers between devices, on_device(): lax.psum_scatter(lax.dot_general(columns, normed, (((0,), (0,)), ((), ())...  53.7 us
    all_gather x1, waiting for transfers between devices, on_device(): lax.all_gather(out_weight, SEQ, axis=0, tiled=True)  29.5 us
    unnamed x2, blocking collectives  20.1 us
    psum x2, blocking collectives, over_axes(): x = lax.psum(x, axis)  18.9 us
    unnamed x32, local copies, waits for them, and re-layouts  13.2 us
    dot_general x1, matrix products, on_device(): jnp.dot(columns, lax.all_gather(out_weight, SEQ, axis=0, tiled=True), pre...  11.3 us
    dot_general x1, matrix products, on_device(): lax.dot_general(columns, normed, (((0,), (0,)), ((), ())), preferred_elem...  11 us
  transfers between devices with their start and end apart: 4, of which 3 were waited for; matrix products, arithmetic and copies ran while one was open for 15% of the time, Pallas kernels for 0%

commit v1 on v0

--- a/solution.py
+++ b/solution.py
@@ -11,6 +11,12 @@
 HEAD = ("head_0", "head_1")
 SEQ = ("seq_0", "seq_1")
 epsilon = 1e-05
+
+
+def _review_object(frame_in, which_axis):
+    return jnp.concatenate(
+        lax.all_to_all(jnp.stack(lax.axis_size(which_axis) * [frame_in]), which_axis, 0, 0), 0
+    )
 
 
 def over_axes(x, axes):
@@ -64,9 +70,7 @@
     local_squares = jnp.sum(gated_values * gated_values, axis=1)
     columns = full_grad
     normed_grad = jnp.dot(
-        columns,
-        lax.all_gather(out_weight, SEQ, axis=0, tiled=True),
-        preferred_element_type=jnp.float32,
+        columns, _review_object(out_weight, SEQ), preferred_element_type=jnp.float32
     )
     squares = over_axes(local_squares, HEAD)
     weighted = over_axes(jnp.sum(norm_weight * normed_grad * gated_values, axis=1), HEAD)

time: 295 us -> 271 us (0.919)
  waiting for transfers between devices: 167 us -> 135 us
  starting transfers between devices: 0.34 us -> 8.92 us
    all_gather x1, waiting for transfers between devices: 82.9 us -> 0.01 us  [on_device(): full_grad = lax.all_gather(grad_output, HEAD, axis=1, tiled=True)]
    all_to_all x0 -> x1, waiting for transfers between devices: none -> 79.8 us  [_review_object(): lax.all_to_all(jnp.stack(lax.axis_size(which_axis) * [frame_in]), which_a...]
    all_gather x1 -> x0, waiting for transfers between devices: 29.5 us -> none  [on_device(): lax.all_gather(out_weight, SEQ, axis=0, tiled=True)]
    all_to_all x0 -> x1, starting transfers between devices: none -> 8.62 us  [_review_object(): lax.all_to_all(jnp.stack(lax.axis_size(which_axis) * [frame_in]), which_a...]
    another operation x2 -> x3, local copies, waits for them, and re-layouts: 0.02 us -> 3.31 us  [the longest x1 3.29 us: _review_object(): jnp.stack(lax.axis_size(which_axis) * [frame_in])]
    unnamed x32 -> x38, local copies, waits for them, and re-layouts: 13.2 us -> 11.9 us
  transfers between devices with their start and end apart: 4 -> 4, of which waited for: 3 -> 2; matrix products, arithmetic and copies ran while one was open for 15% -> 16% of each run, Pallas kernels for 0% -> 0%
where the time goes in v1:
time: 271 us; the launch traced here: 270 us
  waiting for transfers between devices  135 us (50%)
  blocking collectives  39.9 us (15%)
  matrix products  39.5 us (15%)
  other arithmetic  15.8 us (6%)
  local copies, waits for them, and re-layouts  15.7 us (6%)
  between operations  15.3 us (6%)
  starting transfers between devices  8.92 us (3%)
    all_to_all x1, waiting for transfers between devices, _review_object(): lax.all_to_all(jnp.stack(lax.axis_size(which_axis) * [frame_in]), which_a...  79.8 us
    reduce_scatter x1, waiting for transfers between devices, on_device(): lax.psum_scatter(lax.dot_general(columns, normed, (((0,), (0,)), ((), ())...  54.7 us
    psum x2, blocking collectives, over_axes(): x = lax.psum(x, axis)  19.6 us
    unnamed x2, blocking collectives  18.2 us
    unnamed x38, local copies, waits for them, and re-layouts  11.9 us
    dot_general x1, matrix products, on_device(): jnp.dot(columns, _review_object(out_weight, SEQ), preferred_element_type=...  11.3 us
    dot_general x1, matrix products, on_device(): lax.dot_general(columns, normed, (((0,), (0,)), ((), ())), preferred_elem...  11 us
    all_to_all x1, starting transfers between devices, _review_object(): lax.all_to_all(jnp.stack(lax.axis_size(which_axis) * [frame_in]), which_a...  8.62 us
  transfers between devices with their start and end apart: 4, of which 2 were waited for; matrix products, arithmetic and copies ran while one was open for 16% of the time, Pallas kernels for 0%

profile of v1, /device:TPU:2, one launch (start us, length us, event | category | flops | bytes accessed | tf_op | source)
XLA Modules:
  0.0 270.5 jit_solution(18068990527524542839)
XLA Ops:
  7.9 3.3 %stack.2 = bf16[16,256,512]{2,1,0:T(8,128)(2,1)} broadcast(bf16[256,512]{1,0:T(8,128)(2,1)} %param.13), dimensions={1,2} | broadcast | bytes 4456448 | tf_op jit(solution)/shard_map/stack | solution.py:18
  11.2 8.6 %all-to-all-start = ((bf16[16,256,512]{2,1,0:T(8,128)(2,1)}), bf16[16,256,512]{2,1,0:T(8,128)(2,1)}, u32[]{:S(2)}, u32[]{:S(2)}) async-start(bf16[16,256,512]{2,1,0:T(8,128)(2,1)} %stack.2), calls=%async_computation | async-start | bytes 8388608 | tf_op jit(solution)/shard_map/all_to_all | solution.py:18
  19.9 1.5 copy.74
  21.5 2.6 copy.75
  24.1 2.3 reduce-window.6
  29.6 2.5 all-reduce
  32.3 2.1 convolution_convert_fusion.1
  34.4 79.8 %all-to-all-done = bf16[16,256,512]{2,1,0:T(8,128)(2,1)} async-done(((bf16[16,256,512]{2,1,0:T(8,128)(2,1)}), bf16[16,256,512]{2,1,0:T(8,128)(2,1)}, u32[]{:S(2)}, u32[]{:S(2)}) %all-to-all-start) | async-done | bytes 4194336 | tf_op jit(solution)/shard_map/all_to_all | solution.py:18
  114.2 11.3 %multiply_reduce_fusion.1 = (f32[1024]{0:T(1024)S(1)}, f32[1024]{0:T(1024)S(1)}, f32[1024,512]{0,1:T(8,128)}) fusion(bf16[1024,512]{0,1:T(8,128)(2,1)S(1)} %copy.74, bf16[1024,512]{0,1:T(8,128)(2,1)} %copy.75, f32[512]{0:T(512)S(1)} %copy-done.8, bf16[1024,4096]{1,0:T(8,128)(2,1)} %all-gather.6.cloned.1.call-done, bf16[4096,512]{1,0:T(8,128)(2,1)} %bitcast.5), kind=kOutput, calls=%fused_computation.32 | convolution fusion | flops 4301256704 | bytes 16787456 | tf_op jit(solution)/shard_map/dot_general | solution.py:72
  125.5 8.7 %all-reduce.3 = (f32[1024]{0:T(1024)S(1)}, f32[1024]{0:T(1024)S(1)}) all-reduce(f32[1024]{0:T(1024)S(1)} %get-tuple-element.160, f32[1024]{0:T(1024)S(1)} %get-tuple-element.159), channel_id=1, replica_groups=mesh['seq_0'=8,'seq_1'=2,'head_0'=4,'head_1'=4] {'head_0'}, use_global_device_ids=true, to_apply=%region_6.0 | all-reduce | flops 2048 | bytes 16384 | tf_op jit(solution)/shard_map/psum | solution.py:24
  134.2 10.9 %all-reduce.2 = (f32[1024]{0:T(1024)S(1)}, f32[1024]{0:T(1024)S(1)}) all-reduce(f32[1024]{0:T(1024)S(1)} %get-tuple-element.175, f32[1024]{0:T(1024)S(1)} %get-tuple-element.176), channel_id=1, replica_groups=mesh['seq_0'=8,'seq_1'=2,'head_0'=4,'head_1'=4] {'head_1'}, use_global_device_ids=true, to_apply=%region_7.8 | all-reduce | flops 2048 | bytes 16384 | tf_op jit(solution)/shard_map/psum | solution.py:24
  145.1 4.7 %fusion.9 = (bf16[1024,512]{0,1:T(8,128)(2,1)}, bf16[1024,512]{0,1:T(8,128)(2,1)S(1)}) fusion(bf16[1024,512]{0,1:T(8,128)(2,1)S(1)} %copy.74, bf16[1024,512]{0,1:T(8,128)(2,1)} %copy.75, f32[1024]{0:T(1024)S(1)} %get-tuple-element.173, f32[1024]{0:T(1024)S(1)} %get-tuple-element.182, f32[1024,512]{0,1:T(8,128)} %get-tuple-element.195, f32[512]{0:T(512)S(1)} %copy-done.8, ...), kind=kLoop, calls=%fused_computation.20 | loop fusion | flops 11534336 | bytes 6305792 | tf_op jit(solution)/shard_map/convert_element_type | solution.py:85
  149.7 1.8 fusion.27
  151.7 4.5 %while.17 = (s32[]{:T(128)}, f32[8,64,128]{2,1,0:T(8,128)S(1)}, f32[4,8,64,128]{3,2,1,0:T(8,128)S(1)}, f32[4,8,64,128]{3,2,0,1:T(8,128)}, f32[4,8]{1,0:T(4,128)S(1)}, /*index=5*/s32[]{:T(128)}, s32[]{:T(128)}, s32[]{:T(128)}) while((s32[]{:T(128)}, f32[8,64,128]{2,1,0:T(8,128)S(1)}, f32[4,8,64,128]{3,2,1,0:T(8,128)S(1)}, ...), condition=%wide.region_9.10_spmd.clone, body=%wide.region_8.9_spmd.clone.sunk | while | flops 262148 | bytes 1310936 | solution.py:139
  157.2 2.2 all-gather
  160.4 11.0 %fusion.2 = bf16[4096,512]{0,1:T(8,128)(2,1)} fusion(bf16[1024,4096]{1,0:T(8,128)(2,1)} %all-gather.6.cloned.1.call-done, f32[512]{0:T(512)S(1)} %copy-done.8, bf16[1024,512]{0,1:T(8,128)(2,1)} %copy-done.2, f32[1024]{0:T(1024)S(1)} %get-tuple-element.181, bf16[1024,512]{0,1:T(8,128)(2,1)} %copy.75), kind=kOutput, calls=%fused_computation.7 | convolution fusion | flops 4302307328 | bytes 14686208 | tf_op jit(solution)/shard_map/dot_general | solution.py:89
  172.2 15.7 %all-reduce.1 = f32[64]{0:T(128)S(1)} all-reduce(f32[64]{0:T(128)S(1)} %copy-done.11), channel_id=4, replica_groups=mesh['seq_0'=8,'seq_1'=2,'head_0'=4,'head_1'=4] {'seq_0'}, use_global_device_ids=true, to_apply=%add.1 | all-reduce | flops 64 | bytes 512
  188.0 3.7 %convolution_convert_fusion.2 = bf16[8,1024,128]{2,0,1:T(8,128)(2,1)} fusion(bf16[1024,8,128]{2,1,0:T(8,128)(2,1)} %param.19, s32[8]{0:T(128)S(1)} %and_select_fusion), kind=kOutput, calls=%fused_computation.34 | convolution fusion | flops 17825856 | bytes 4194336 | tf_op jit(solution)/shard_map/tgn,hg->htn/dot_general | solution.py:108
  191.6 2.3 copy.86
  193.9 6.4 %fusion.3 = f32[8,4,256,64]{2,3,1,0:T(8,128)} fusion(f32[8,4,256]{2,1,0:T(4,128)S(1)} %copy.72, pred[256,256]{1,0:T(8,128)(4,1)S(1)} %iota_compare_fusion, bf16[8,4,256,128]{3,0,2,1:T(8,128)(2,1)} %bitcast.137, bf16[8,4,256,128]{3,0,2,1:T(8,128)(2,1)} %bitcast.131, bf16[8,8,4,8,256]{4,3,2,1,0:T(8,128)(2,1)} %bitcast.134), kind=kOutput, calls=%fused_computation.8 | convolution fusion | flops 815792128 | bytes 7438336 | tf_op jit(solution)/shard_map/hkts,hksp->hktp/dot_general | solution.py:127
  200.3 2.1 fusion.53
  202.5 3.3 %fusion.30 = bf16[8,4,8,8,256]{4,3,2,1,0:T(8,128)(2,1)S(1)} fusion(f32[8,4,256,64]{2,3,1,0:T(8,128)} %fusion.3, bf16[8,4,256,128]{3,0,2,1:T(8,128)(2,1)S(1)} %bitcast.132, f32[8]{0:T(128)S(1)} %copy-done.9, f32[8,4,256]{2,1,0:T(4,128)S(1)} %copy.83, f32[8,4,256]{2,1,0:T(4,128)S(1)} %copy.67, bf16[8,8,4,8,256]{4,3,2,1,0:T(8,128)(2,1)} %bitcast.135, ...), kind=kOutput, calls=%fused_computation.42 | convolution fusion | flops 138674176 | bytes 7667872 | tf_op jit(solution)/shard_map/hkpn,hktn->hktp/dot_general | solution.py:155
  206.0 1.3 copy.85
  207.3 54.7 %reduce-scatter.2.cloned.1.call-done = bf16[256,512]{0,1:T(8,128)(2,1)} async-done(((bf16[4096,512]{0,1:T(8,128)(2,1)}), bf16[256,512]{0,1:T(8,128)(2,1)}) %reduce-scatter.2.cloned.1.call-update) | async-done | bytes 262160 | tf_op jit(solution)/shard_map/reduce_scatter | solution.py:88
  (77 shorter events, 12.5 us)
Async XLA Ops:
  7.2 25.1 %copy-start = (bf16[1024,8,128]{2,1,0:T(8,128)(2,1)S(1)}, bf16[1024,8,128]{2,1,0:T(8,128)(2,1)}, u32[]{:S(2)}) copy-start(bf16[1024,8,128]{2,1,0:T(8,128)(2,1)} %param.20) | copy-start | bytes 6291460
  7.2 107.0 %all-gather.6.cloned.1.call-start = ((), (), s32[]{:S(2)}) async-start(), calls=%async_computation.2 | async-start | bytes 8912896 | tf_op jit(solution)/shard_map/all_gather | solution.py:64
  11.2 103.0 %all-to-all-start = ((bf16[16,256,512]{2,1,0:T(8,128)(2,1)}), bf16[16,256,512]{2,1,0:T(8,128)(2,1)}, u32[]{:S(2)}, u32[]{:S(2)}) async-start(bf16[16,256,512]{2,1,0:T(8,128)(2,1)} %stack.2), calls=%async_computation | async-start | bytes 8388608 | tf_op jit(solution)/shard_map/all_to_all | solution.py:18
  19.8 180.4 %all-gather.8.cloned.1.call-start = ((), (), s32[]{:S(2)}) async-start(), calls=%async_computation.3 | async-start | bytes 2359296 | tf_op jit(solution)/shard_map/all_gather | solution.py:39
  19.9 4.2 %copy-start.6 = (f32[8,1024]{1,0:T(8,128)S(1)}, f32[8,1024]{1,0:T(8,128)}, u32[]{:S(2)}) copy-start(f32[8,1024]{1,0:T(8,128)} %param.18) | copy-start | bytes 98308
  19.9 7.1 %copy-start.13 = (u32[256]{0:T(256)S(1)}, u32[256]{0:T(256)}, u32[]{:S(2)}) copy-start(u32[256]{0:T(256)} %constant.117) | copy-start | bytes 3076
  19.9 7.7 %copy-start.12 = (u32[256]{0:T(256)S(1)}, u32[256]{0:T(256)}, u32[]{:S(2)}) copy-start(u32[256]{0:T(256)} %constant.122) | copy-start | bytes 3076
  21.4 123.6 %copy-start.2 = (bf16[1024,512]{0,1:T(8,128)(2,1)}, bf16[1024,512]{0,1:T(8,128)(2,1)S(1)}, u32[]{:S(2)}) copy-start(bf16[1024,512]{0,1:T(8,128)(2,1)S(1)} %copy.74) | copy-start | bytes 3145732
  32.3 2.1 copy-start.10
  32.3 81.9 %copy-start.8 = (f32[512]{0:T(512)S(1)}, f32[512]{0:T(512)}, u32[]{:S(2)}) copy-start(f32[512]{0:T(512)} %param.16) | copy-start | bytes 6148
  145.1 4.7 %copy-start.5 = (bf16[8,1024,128]{2,0,1:T(8,128)(2,1)S(1)}, bf16[8,1024,128]{2,0,1:T(8,128)(2,1)}, u32[]{:S(2)}) copy-start(bf16[8,1024,128]{2,0,1:T(8,128)(2,1)} %convolution_convert_fusion.1) | copy-start | bytes 6291460
  149.7 1.8 copy-start.3
  156.2 1.0 copy-start.4
  160.2 101.8 %reduce-scatter.2.cloned.1.call-start = ((), (), s32[]{:S(2)}) async-start(), calls=%async_computation.4 | async-start | bytes 4456448 | tf_op jit(solution)/shard_map/reduce_scatter | solution.py:88
  171.4 0.8 copy-start.7
  171.4 0.8 copy-start.11
  200.3 2.1 copy-start.9
  200.3 2.2 copy-start.1
Sparse Core Ops, SparseCore 0:
  10.4 84.9 all-gather.5
  160.3 37.3 all-gather.7
  200.2 61.6 reduce-scatter.1
